TPU v7x, 256 devices: a whole 4x4x8 slice. The times are simulated.
256 devices in a mesh: seq: 32 (over y, z), tp: 8 (over x, core).
Axes of the slice: x: 4, y: 4, z: 8, core: 2. Of those that a mesh axis runs over, the one named last changes fastest.
Arguments:
- tokens: bfloat16 [24576, 2048], P('seq', 'tp'), may hold values from -20 to 20
- w_query: bfloat16 [2048, 2048], P(None, 'tp'), may hold values from -0.125 to 0.125
- w_key: bfloat16 [2048, 2048], P(None, 'tp'), may hold values from -0.125 to 0.125
- w_value: bfloat16 [2048, 2048], P(None, 'tp'), may hold values from -0.125 to 0.125
- head_gain: float32 [2048], P('tp'), may hold values from 0.5 to 1.5
- w_out: bfloat16 [2048, 2048], P('tp'), may hold values from -0.125 to 0.125
- norm_gain: float32 [2048], replicated, may hold values from 0.5 to 1.5
- w_gate: bfloat16 [2048, 8192], P('seq', 'tp'), may hold values from -0.125 to 0.125
- w_up: bfloat16 [2048, 8192], P('seq', 'tp'), may hold values from -0.125 to 0.125
- w_down: bfloat16 [8192, 2048], P('tp', 'seq'), may hold values from -0.0625 to 0.0625
Outputs:
- layer_out: bfloat16 [24576, 2048], P('seq', 'tp')
All inputs are finite; a program needn't handle non-finite values.
Results may differ from a plain program's by a relative error of at most 0.009.
Values may be sent and summed in bfloat16 or wider, within the bound.
No kernel may reach another device: no remote copies, remote signals or barrier semaphores. Data moves between devices by JAX's collectives and lax.ppermute only.
A program may use at most 128 MiB of HBM per device.

v0:
```python
import jax
import jax.numpy as jnp
from jax import lax
from jax.sharding import Mesh
from jax.sharding import PartitionSpec as P

HD = 128
SEQ = ("seq_0", "seq_1")


def nothing_yet(array, identity):
    return jnp.zeros_like(array) + jnp.asarray(identity, array.dtype)


def entering(array, axes, combine, identity):
    before = start = nothing_yet(array, identity)
    total = array
    for axis in reversed(axes):
        peers, position = (lax.axis_size(axis), lax.axis_index(axis))
        pieces = lax.all_gather(total.astype(jnp.bfloat16), axis)
        inside, total = (start, start)
        for k in range(peers):
            passed = k < position
            total = combine(total, pieces[k].astype(array.dtype))
            inside = jnp.where(passed, total, inside)
        before = combine(inside, before)
    return before


def in_one_piece(arrays, axis, dim, along):
    ends, at = ([], 0)
    for a in arrays[:-1]:
        at += a.shape[along]
        ends.append(at)
    both = jnp.concatenate(arrays, axis=along)
    return tuple(jnp.split(lax.all_gather(both, axis, axis=dim, tiled=True), ends, axis=along))


def split_up(array, dim, peers):
    shape = array.shape
    tiles = array.reshape(*shape[:dim], peers, shape[dim] // peers, *shape[dim + 1 :])
    return jnp.moveaxis(tiles, dim, 0)


def sum_at_owner(array, axis, dim):
    tiles = split_up(array, dim, lax.axis_size(axis))
    arrived = lax.all_to_all(tiles, axis, split_axis=0, concat_axis=0, tiled=True)
    return arrived.astype(jnp.float32).sum(axis=0)


def add_states(earlier, later):
    return earlier + later


def body(tokens, w_query, w_key, w_value, head_gain, w_out, norm_gain, w_gate, w_up, w_down):
    length = tokens.shape[0]
    width_here = tokens.shape[1]
    heads_here = w_query.shape[1] // HD
    features = lax.all_gather(tokens, "tp", axis=1, tiled=True)

    def project(weight):
        product = jnp.dot(features, weight, preferred_element_type=jnp.float32)
        return product.astype(jnp.bfloat16).reshape(length, heads_here, HD)

    query = project(w_query)
    keys_local = project(w_key)
    values_local = project(w_value)
    scores = jnp.einsum("ihd,jhd->hij", query, keys_local, preferred_element_type=jnp.float32)
    causal = jnp.arange(length)[:, None] >= jnp.arange(length)[None, :]
    scores = jnp.where(causal[None], scores, 0.0).astype(jnp.bfloat16)
    inside = jnp.einsum("hij,jhd->ihd", scores, values_local, preferred_element_type=jnp.float32)
    own_state = jnp.einsum(
        "jhd,jhe->hde", keys_local, values_local, preferred_element_type=jnp.float32
    )
    history = entering(own_state, SEQ, add_states, jnp.zeros_like(own_state))
    carried = jnp.einsum(
        "ihd,hde->ihe", query, history.astype(jnp.bfloat16), preferred_element_type=jnp.float32
    )
    mixed = inside + carried
    scale = lax.rsqrt(jnp.mean(mixed * mixed, axis=-1, keepdims=True) + 1e-06)
    normed = (mixed * scale * head_gain.reshape(heads_here, HD)).astype(jnp.bfloat16)
    normed = normed.reshape(length, heads_here * HD)
    partial_value = jnp.dot(normed, w_out, preferred_element_type=jnp.float32)
    own_column = lax.axis_index("tp") * width_here
    summed = lax.psum(partial_value.astype(jnp.bfloat16), "tp").astype(jnp.float32)
    resid_whole = features.astype(jnp.float32) + summed
    factor = lax.rsqrt(jnp.mean(resid_whole * resid_whole, axis=-1, keepdims=True) + 1e-05)
    ffn_in = (resid_whole * factor * norm_gain).astype(jnp.bfloat16)
    resid = lax.dynamic_slice_in_dim(resid_whole, own_column, width_here, 1)
    pieces = in_one_piece((w_gate, w_up), SEQ, 0, 1)
    gate_sum = jnp.dot(ffn_in, pieces[0], preferred_element_type=jnp.float32)
    upward_sum = jnp.dot(ffn_in, pieces[1], preferred_element_type=jnp.float32)
    hidden = (jax.nn.silu(gate_sum) * upward_sum).astype(jnp.bfloat16)
    terms = jnp.dot(
        hidden, lax.all_gather(w_down, SEQ, axis=1, tiled=True), preferred_element_type=jnp.float32
    )
    mlp_share = sum_at_owner(terms.astype(jnp.bfloat16), "tp", 1)
    return (resid + mlp_share).astype(jnp.bfloat16)


def solution(mesh):
    finer = Mesh(mesh.devices.reshape(4, 8, mesh.shape["tp"]), ("seq_0", "seq_1", "tp"))
    return jax.shard_map(
        body,
        mesh=finer,
        in_specs=(
            P(SEQ, "tp"),
            P(None, "tp"),
            P(None, "tp"),
            P(None, "tp"),
            P("tp"),
            P("tp", None),
            P(),
            P(SEQ, "tp"),
            P(SEQ, "tp"),
            P("tp", SEQ),
        ),
        out_specs=P(SEQ, "tp"),
        check_vma=False,
    )
```

profile of v0, /device:TPU:1, one launch (start us, length us, event | category | flops | bytes accessed | tf_op | source)
XLA Modules:
  0.0 356.1 jit_solution(3774338087254047791)
XLA Ops:
  7.4 0.7 all-gather.5.cloned.1.call-update
  8.3 39.5 %all-gather.5.cloned.1.call-done = bf16[768,2048]{1,0:T(8,128)(2,1)} async-done(((bf16[768,256]{1,0:T(8,128)(2,1)}), bf16[768,2048]{1,0:T(8,128)(2,1)}) %all-gather.5.cloned.1.call-update) | async-done | bytes 3145744 | tf_op jit(solution)/shard_map/all_gather | solution.py:59
  47.9 3.3 convolution_convert_fusion.2
  51.2 2.4 convolution_convert_fusion.4
  53.9 20.8 %all-gather = bf16[16,128,128]{2,1,0:T(8,128)(2,1)S(1)} all-gather(bf16[2,128,128]{2,1,0:T(8,128)(2,1)S(1)} %convolution_convert_fusion.5), channel_id=2, replica_groups=mesh['seq_0'=4,'seq_1'=8,'tp'=8] {'seq_1'}, dimensions={0}, use_global_device_ids=true | all-gather | bytes 589824 | tf_op jit(solution)/shard_map/all_gather | solution.py:20
  74.7 9.7 %all_gather.22 = bf16[4,2,128,128]{3,2,1,0:T(8,128)(2,1)S(1)} all-gather(bf16[1,2,128,128]{3,2,1,0:T(8,128)(2,1)S(1)} %fusion.28), channel_id=1, replica_groups=mesh['seq_0'=4,'seq_1'=8,'tp'=8] {'seq_0'}, dimensions={0}, use_global_device_ids=true | all-gather | bytes 327680 | tf_op jit(solution)/shard_map/all_gather | solution.py:20
  84.5 1.1 convolution_convert_fusion.3
  85.6 0.7 copy-done.7
  86.3 1.3 fusion.29
  87.6 2.9 multiply_reduce_fusion.1
  90.6 2.7 convolution_convert_fusion.1
  93.5 0.8 copy-done.2
  94.3 0.7 pad_maximum_fusion
  95.7 79.1 %all-reduce.2.cloned.1.call-done = bf16[768,2048]{1,0:T(8,128)(2,1)} async-done(((bf16[768,2048]{1,0:T(8,128)(2,1)}), bf16[768,2048]{1,0:T(8,128)(2,1)}) %all-reduce.2.cloned.1.call-update) | async-done | bytes 3145744 | tf_op jit(solution)/shard_map/psum | solution.py:85
  174.8 6.7 %convert_add_fusion = (f32[768,2048]{1,0:T(8,128)}, f32[768]{0:T(1024)S(1)}) fusion(bf16[768,2048]{1,0:T(8,128)(2,1)} %all-reduce.2.cloned.1.call-done, bf16[768,2048]{1,0:T(8,128)(2,1)} %all-gather.5.cloned.1.call-done), kind=kLoop, calls=%fused_computation.3 | loop fusion | flops 7863552 | bytes 12585984 | tf_op jit(solution)/shard_map/add | solution.py:86
  181.6 19.3 %all-gather.7.cloned.1.call-done = bf16[2048,2048]{1,0:T(8,128)(2,1)} async-done(((bf16[64,2048]{1,0:T(8,128)(2,1)}), bf16[2048,2048]{1,0:T(8,128)(2,1)}) %all-gather.7.cloned.1.call-update) | async-done | bytes 8388624 | tf_op jit(solution)/shard_map/all_gather | solution.py:36
  200.9 9.2 %fusion = f32[768,1024]{1,0:T(8,128)} fusion(bf16[2048,2048]{1,0:T(8,128)(2,1)} %all-gather.7.cloned.1.call-done, f32[2048]{0:T(1024)S(1)} %copy-done.6, f32[768]{0:T(1024)S(1)} %add_rsqrt_fusion.1, bf16[768,2048]{1,0:T(8,128)(2,1)} %all-reduce.2.cloned.1.call-done, bf16[768,2048]{1,0:T(8,128)(2,1)} %all-gather.5.cloned.1.call-done), kind=kOutput, calls=%fused_computation.5 | convolution fusion | flops 3230662656 | bytes 13642752 | tf_op jit(solution)/shard_map/dot_general | solution.py:92
  210.2 69.3 %all-gather.9.cloned.1.call-done = bf16[1024,2048]{0,1:T(8,128)(2,1)} async-done(((bf16[1024,64]{0,1:T(8,128)(2,1)}), bf16[1024,2048]{0,1:T(8,128)(2,1)}) %all-gather.9.cloned.1.call-update) | async-done | bytes 4194320 | tf_op jit(solution)/shard_map/all_gather | solution.py:95
  279.5 14.9 %convolution_convert_fusion = bf16[768,2048]{1,0:T(8,128)(2,1)} fusion(bf16[1024,2048]{0,1:T(8,128)(2,1)} %all-gather.9.cloned.1.call-done, f32[768,1024]{1,0:T(8,128)} %fusion, bf16[2048,2048]{1,0:T(8,128)(2,1)} %all-gather.7.cloned.1.call-done, f32[2048]{0:T(1024)S(1)} %copy-done.6, f32[768]{0:T(1024)S(1)} %add_rsqrt_fusion.1, ...), kind=kOutput, calls=%fused_computation.9 | convolution fusion | flops 6458179584 | bytes 20982784 | tf_op jit(solution)/shard_map/dot_general | solution.py:94
  294.4 3.7 %copy.23 = bf16[96,8,8,256]{3,2,0,1:T(8,128)(2,1)} copy(bf16[96,8,8,256]{3,2,1,0:T(8,128)(2,1)} %bitcast.58) | data formatting | bytes 6291456 | tf_op jit(solution)/shard_map/reshape | solution.py:41
  298.1 8.6 %all-to-all-start = ((bf16[8,768,256]{2,1,0:T(8,128)(2,1)}), bf16[8,768,256]{2,1,0:T(8,128)(2,1)}, u32[]{:S(2)}, u32[]{:S(2)}) async-start(bf16[8,768,256]{2,1,0:T(8,128)(2,1)} %bitcast.57), calls=%async_computation | async-start | bytes 6291456 | tf_op jit(solution)/shard_map/all_to_all | solution.py:47
  306.7 37.6 %all-to-all-done = bf16[8,768,256]{2,1,0:T(8,128)(2,1)} async-done(((bf16[8,768,256]{2,1,0:T(8,128)(2,1)}), bf16[8,768,256]{2,1,0:T(8,128)(2,1)}, u32[]{:S(2)}, u32[]{:S(2)}) %all-to-all-start) | async-done | bytes 3145760 | tf_op jit(solution)/shard_map/all_to_all | solution.py:47
  344.3 2.4 convert_reduce_fusion
  346.7 2.0 add_convert_fusion
  (27 shorter events, 1.4 us)
Async XLA Ops:
  7.4 83.3 %copy-start = (bf16[256,2048]{1,0:T(8,128)(2,1)S(1)}, bf16[256,2048]{1,0:T(8,128)(2,1)}, u32[]{:S(2)}) copy-start(bf16[256,2048]{1,0:T(8,128)(2,1)} %param.15) | copy-start | bytes 3145732
  7.4 40.5 %all-gather.5.cloned.1.call-start = ((), (), s32[]{:S(2)}) async-start(), calls=%async_computation.1 | async-start | bytes 3538944 | tf_op jit(solution)/shard_map/all_gather | solution.py:59
  8.1 166.7 %all-reduce.2.cloned.1.call-start = ((), (), s32[]{:S(2)}) async-start(), calls=%async_computation.2 | async-start | bytes 6291456 | tf_op jit(solution)/shard_map/psum | solution.py:85
  47.9 3.4 copy-start.1
  51.2 33.2 %copy-start.5 = (bf16[2048,256]{1,0:T(8,128)(2,1)S(1)}, bf16[2048,256]{1,0:T(8,128)(2,1)}, u32[]{:S(2)}) copy-start(bf16[2048,256]{1,0:T(8,128)(2,1)} %param.11) | copy-start | bytes 3145732
  85.6 0.7 copy-start.7
  87.6 2.9 copy-start.4
  93.4 0.9 copy-start.2
  93.4 1.0 copy-start.3
  93.4 107.5 %all-gather.7.cloned.1.call-start = ((), (), s32[]{:S(2)}) async-start(), calls=%async_computation.3 | async-start | bytes 8650752 | tf_op jit(solution)/shard_map/all_gather | solution.py:36
  95.1 184.4 %all-gather.9.cloned.1.call-start = ((), (), s32[]{:S(2)}) async-start(), calls=%async_computation.4 | async-start | bytes 4325376 | tf_op jit(solution)/shard_map/all_gather | solution.py:95
  95.7 105.2 %copy-start.6 = (f32[2048]{0:T(1024)S(1)}, f32[2048]{0:T(1024)}, u32[]{:S(2)}) copy-start(f32[2048]{0:T(1024)} %param.16) | copy-start | bytes 24580
  298.1 46.2 %all-to-all-start = ((bf16[8,768,256]{2,1,0:T(8,128)(2,1)}), bf16[8,768,256]{2,1,0:T(8,128)(2,1)}, u32[]{:S(2)}, u32[]{:S(2)}) async-start(bf16[8,768,256]{2,1,0:T(8,128)(2,1)} %bitcast.57), calls=%async_computation | async-start | bytes 6291456 | tf_op jit(solution)/shard_map/all_to_all | solution.py:47
Sparse Core Ops, SparseCore 0:
  10.0 37.8 all-gather.4
  93.5 81.2 all-reduce.1
Sparse Core Ops, SparseCore 1:
  96.5 104.4 all-gather.6
  203.4 76.1 all-gather.8
where the time goes:
time: 356 us
  waiting for transfers between devices  246 us (69%)
  matrix products  38.1 us (11%)
  blocking collectives  30.5 us (9%)
  between operations  15 us (4%)
  other arithmetic  12.2 us (3%)
  starting transfers between devices  8.92 us (3%)
  local copies, waits for them, and re-layouts  5.37 us (2%)
    psum x1, waiting for transfers between devices, body(): lax.psum(partial_value.astype(jnp.bfloat16), 'tp').astype(jnp.float32)  79.1 us
    all_gather x1, waiting for transfers between devices, body(): lax.all_gather(w_down, SEQ, axis=1, tiled=True)  69.3 us
    all_gather x1, waiting for transfers between devices, body(): features = lax.all_gather(tokens, 'tp', axis=1, tiled=True)  39.5 us
    all_to_all x1, waiting for transfers between devices, sum_at_owner(): lax.all_to_all(tiles, axis, split_axis=0, concat_axis=0, tiled=True)  37.6 us
    all_gather x2, blocking collectives, entering(): pieces = lax.all_gather(total.astype(jnp.bfloat16), axis)  30.5 us
    all_gather x1, waiting for transfers between devices, in_one_piece(): lax.all_gather(both, axis, axis=dim, tiled=True)  19.3 us
    dot_general x1, matrix products, body(): jnp.dot(hidden, lax.all_gather(w_down, SEQ, axis=1, tiled=True), preferre...  14.9 us
    dot_general x1, matrix products, body(): upward_sum = jnp.dot(ffn_in, pieces[1], preferred_element_type=jnp.float32)  9.24 us
  transfers between devices with their start and end apart: 5, of which 5 were waited for; matrix products, arithmetic and copies ran while one was open for 5% of the time, Pallas kernels for 0%

commit v1 on v0

--- a/solution.py
+++ b/solution.py
@@ -56,7 +56,8 @@
     length = tokens.shape[0]
     width_here = tokens.shape[1]
     heads_here = w_query.shape[1] // HD
-    features = lax.all_gather(tokens, "tp", axis=1, tiled=True)
+    parts = lax.all_gather(tokens, "tp")
+    features = jnp.concatenate(parts, axis=1)
 
     def project(weight):
         product = jnp.dot(features, weight, preferred_element_type=jnp.float32)

time: 356 us -> 351 us (0.986)
  waiting for transfers between devices: 246 us -> 242 us
  matrix products: 38.1 us -> 34.4 us
    dot_general x3, matrix products: 6.82 us -> 3.09 us  [project(): product = jnp.dot(features, weight, preferred_element_type=jnp.float32)]
where the time goes in v1:
time: 351 us
  waiting for transfers between devices  242 us (69%)
  matrix products  34.4 us (10%)
  blocking collectives  30.5 us (9%)
  between operations  15 us (4%)
  other arithmetic  12.3 us (4%)
  starting transfers between devices  8.94 us (3%)
  local copies, waits for them, and re-layouts  8.15 us (2%)
    psum x1, waiting for transfers between devices, body(): lax.psum(partial_value.astype(jnp.bfloat16), 'tp').astype(jnp.float32)  77.9 us
    all_gather x1, waiting for transfers between devices, body(): lax.all_gather(w_down, SEQ, axis=1, tiled=True)  69.3 us
    all_to_all x1, waiting for transfers between devices, sum_at_owner(): lax.all_to_all(tiles, axis, split_axis=0, concat_axis=0, tiled=True)  37.6 us
    all_gather x1, waiting for transfers between devices, body(): parts = lax.all_gather(tokens, 'tp')  36.1 us
    all_gather x2, blocking collectives, entering(): pieces = lax.all_gather(total.astype(jnp.bfloat16), axis)  30.5 us
    all_gather x1, waiting for transfers between devices, in_one_piece(): lax.all_gather(both, axis, axis=dim, tiled=True)  19.6 us
    dot_general x1, matrix products, body(): jnp.dot(hidden, lax.all_gather(w_down, SEQ, axis=1, tiled=True), preferre...  14.9 us
    dot_general x1, matrix products, body(): upward_sum = jnp.dot(ffn_in, pieces[1], preferred_element_type=jnp.float32)  9.25 us
  transfers between devices with their start and end apart: 5, of which 5 were waited for; matrix products, arithmetic and copies ran while one was open for 5% of the time, Pallas kernels for 0%

profile of v1, /device:TPU:1, one launch (start us, length us, event | category | flops | bytes accessed | tf_op | source)
XLA Modules:
  0.0 350.8 jit_solution(10659116007552938657)
XLA Ops:
  8.3 36.1 %all-gather.10.cloned.1.call-done = bf16[6144,256]{1,0:T(8,128)(2,1)} async-done(((bf16[768,256]{1,0:T(8,128)(2,1)}), bf16[6144,256]{1,0:T(8,128)(2,1)}) %all-gather.10.cloned.1.call-update) | async-done | bytes 3145744 | tf_op jit(solution)/shard_map/all_gather | solution.py:59
  44.4 2.4 copy.24
  46.9 1.0 convolution_convert_fusion.2
  47.9 0.9 copy-done.6
  48.8 1.0 convolution_convert_fusion.3
  50.1 1.0 convolution_convert_fusion.4
  51.4 20.8 %all-gather.1 = bf16[16,128,128]{2,1,0:T(8,128)(2,1)S(1)} all-gather(bf16[2,128,128]{2,1,0:T(8,128)(2,1)S(1)} %convolution_convert_fusion.5), channel_id=3, replica_groups=mesh['seq_0'=4,'seq_1'=8,'tp'=8] {'seq_1'}, dimensions={0}, use_global_device_ids=true | all-gather | bytes 589824 | tf_op jit(solution)/shard_map/all_gather | solution.py:20
  72.2 9.7 %all_gather.26 = bf16[4,2,128,128]{3,2,1,0:T(8,128)(2,1)S(1)} all-gather(bf16[1,2,128,128]{3,2,1,0:T(8,128)(2,1)S(1)} %fusion.28), channel_id=1, replica_groups=mesh['seq_0'=4,'seq_1'=8,'tp'=8] {'seq_0'}, dimensions={0}, use_global_device_ids=true | all-gather | bytes 327680 | tf_op jit(solution)/shard_map/all_gather | solution.py:20
  81.9 1.3 fusion.29
  83.2 2.9 multiply_reduce_fusion.1
  86.3 2.8 convolution_convert_fusion.1
  89.1 0.8 copy-done.2
  90.0 0.7 pad_maximum_fusion
  91.4 77.9 %all-reduce.2.cloned.1.call-done = bf16[768,2048]{1,0:T(8,128)(2,1)} async-done(((bf16[768,2048]{1,0:T(8,128)(2,1)}), bf16[768,2048]{1,0:T(8,128)(2,1)}) %all-reduce.2.cloned.1.call-update) | async-done | bytes 3145744 | tf_op jit(solution)/shard_map/psum | solution.py:86
  169.2 6.8 %convert_add_fusion = (f32[768,2048]{1,0:T(8,128)}, f32[768]{0:T(1024)S(1)}) fusion(bf16[768,2048]{1,0:T(8,128)(2,1)} %all-reduce.2.cloned.1.call-done, bf16[768,2048]{1,0:T(8,128)(2,1)} %bitcast.67), kind=kLoop, calls=%fused_computation.3 | loop fusion | flops 7863552 | bytes 12585984 | tf_op jit(solution)/shard_map/add | solution.py:87
  176.0 19.6 %all-gather.6.cloned.1.call-done = bf16[2048,2048]{1,0:T(8,128)(2,1)} async-done(((bf16[64,2048]{1,0:T(8,128)(2,1)}), bf16[2048,2048]{1,0:T(8,128)(2,1)}) %all-gather.6.cloned.1.call-update) | async-done | bytes 8388624 | tf_op jit(solution)/shard_map/all_gather | solution.py:36
  195.6 9.3 %fusion = f32[768,1024]{1,0:T(8,128)} fusion(bf16[2048,2048]{1,0:T(8,128)(2,1)} %all-gather.6.cloned.1.call-done, f32[2048]{0:T(1024)S(1)} %copy-done.8, f32[768]{0:T(1024)S(1)} %add_rsqrt_fusion.1, bf16[768,2048]{1,0:T(8,128)(2,1)} %all-reduce.2.cloned.1.call-done, bf16[768,2048]{1,0:T(8,128)(2,1)} %bitcast.68), kind=kOutput, calls=%fused_computation.5 | convolution fusion | flops 3230662656 | bytes 13642752 | tf_op jit(solution)/shard_map/dot_general | solution.py:93
  204.8 69.3 %all-gather.8.cloned.1.call-done = bf16[1024,2048]{0,1:T(8,128)(2,1)} async-done(((bf16[1024,64]{0,1:T(8,128)(2,1)}), bf16[1024,2048]{0,1:T(8,128)(2,1)}) %all-gather.8.cloned.1.call-update) | async-done | bytes 4194320 | tf_op jit(solution)/shard_map/all_gather | solution.py:96
  274.2 14.9 %convolution_convert_fusion = bf16[768,2048]{1,0:T(8,128)(2,1)} fusion(bf16[1024,2048]{0,1:T(8,128)(2,1)} %all-gather.8.cloned.1.call-done, f32[768,1024]{1,0:T(8,128)} %fusion, bf16[2048,2048]{1,0:T(8,128)(2,1)} %all-gather.6.cloned.1.call-done, f32[2048]{0:T(1024)S(1)} %copy-done.8, f32[768]{0:T(1024)S(1)} %add_rsqrt_fusion.1, ...), kind=kOutput, calls=%fused_computation.9 | convolution fusion | flops 6458179584 | bytes 20982784 | tf_op jit(solution)/shard_map/dot_general | solution.py:95
  289.0 3.7 %copy.27 = bf16[96,8,8,256]{3,2,0,1:T(8,128)(2,1)} copy(bf16[96,8,8,256]{3,2,1,0:T(8,128)(2,1)} %bitcast.71) | data formatting | bytes 6291456 | tf_op jit(solution)/shard_map/reshape | solution.py:41
  292.7 8.6 %all-to-all-start = ((bf16[8,768,256]{2,1,0:T(8,128)(2,1)}), bf16[8,768,256]{2,1,0:T(8,128)(2,1)}, u32[]{:S(2)}, u32[]{:S(2)}) async-start(bf16[8,768,256]{2,1,0:T(8,128)(2,1)} %bitcast.63), calls=%async_computation | async-start | bytes 6291456 | tf_op jit(solution)/shard_map/all_to_all | solution.py:47
  301.4 37.6 %all-to-all-done = bf16[8,768,256]{2,1,0:T(8,128)(2,1)} async-done(((bf16[8,768,256]{2,1,0:T(8,128)(2,1)}), bf16[8,768,256]{2,1,0:T(8,128)(2,1)}, u32[]{:S(2)}, u32[]{:S(2)}) %all-to-all-start) | async-done | bytes 3145760 | tf_op jit(solution)/shard_map/all_to_all | solution.py:47
  338.9 2.4 convert_reduce_fusion
  341.3 2.0 add_convert_fusion
  (32 shorter events, 2.3 us)
Async XLA Ops:
  7.4 78.9 %copy-start = (bf16[256,2048]{1,0:T(8,128)(2,1)S(1)}, bf16[256,2048]{1,0:T(8,128)(2,1)}, u32[]{:S(2)}) copy-start(bf16[256,2048]{1,0:T(8,128)(2,1)} %param.15) | copy-start | bytes 3145732
  7.4 37.1 %all-gather.10.cloned.1.call-start = ((), (), s32[]{:S(2)}) async-start(), calls=%async_computation.4 | async-start | bytes 3538944 | tf_op jit(solution)/shard_map/all_gather | solution.py:59
  8.1 161.1 %all-reduce.2.cloned.1.call-start = ((), (), s32[]{:S(2)}) async-start(), calls=%async_computation.1 | async-start | bytes 6291456 | tf_op jit(solution)/shard_map/psum | solution.py:86
  44.4 2.4 copy-start.5
  46.8 3.0 copy-start.1
  46.8 2.0 copy-start.6
  48.8 1.2 copy-start.7
  50.1 31.9 %copy-start.9 = (bf16[768,256]{0,1:T(8,128)(2,1)}, bf16[768,256]{0,1:T(8,128)(2,1)S(1)}, u32[]{:S(2)}) copy-start(bf16[768,256]{0,1:T(8,128)(2,1)S(1)} %convolution_convert_fusion.3) | copy-start | bytes 1179652
  83.2 2.9 copy-start.4
  89.0 0.9 copy-start.2
  89.0 1.0 copy-start.3
  89.1 106.5 %all-gather.6.cloned.1.call-start = ((), (), s32[]{:S(2)}) async-start(), calls=%async_computation.2 | async-start | bytes 8650752 | tf_op jit(solution)/shard_map/all_gather | solution.py:36
  90.8 183.4 %all-gather.8.cloned.1.call-start = ((), (), s32[]{:S(2)}) async-start(), calls=%async_computation.3 | async-start | bytes 4325376 | tf_op jit(solution)/shard_map/all_gather | solution.py:96
  91.3 104.2 %copy-start.8 = (f32[2048]{0:T(1024)S(1)}, f32[2048]{0:T(1024)}, u32[]{:S(2)}) copy-start(f32[2048]{0:T(1024)} %param.16) | copy-start | bytes 24580
  292.7 46.2 %all-to-all-start = ((bf16[8,768,256]{2,1,0:T(8,128)(2,1)}), bf16[8,768,256]{2,1,0:T(8,128)(2,1)}, u32[]{:S(2)}, u32[]{:S(2)}) async-start(bf16[8,768,256]{2,1,0:T(8,128)(2,1)} %bitcast.63), calls=%async_computation | async-start | bytes 6291456 | tf_op jit(solution)/shard_map/all_to_all | solution.py:47
Sparse Core Ops, SparseCore 0:
  10.0 34.3 all-gather.9
  89.2 79.9 all-reduce.1
Sparse Core Ops, SparseCore 1:
  92.1 103.4 all-gather.5
  198.0 76.1 all-gather.7
